TPU v7x, 256 devices: a whole 4x4x8 slice. The times are simulated.
256 devices in a mesh: row: 8 (over x, z_lo), col: 8 (over z_hi, core), depth: 4 (over y).
Axes of the slice: x: 4, y: 4, z: 8 (z_hi: 4, z_lo: 2; z = z_hi * 2 + z_lo), core: 2. Of those that a mesh axis runs over, the one named last changes fastest.
Arguments:
- alignment_matrix: bfloat16 [128, 768, 256], P('depth', 'col'), may hold values from -6 to 6
- twin_linear_matrix: bfloat16 [256, 64], replicated, may hold values from -0.375 to 0.375
- final_matrix: bfloat16 [1024, 128], replicated, may hold values from -2 to 2
- final_offset: float32 [128], replicated, may hold values from -3 to 3
- adjoint_incoming: bfloat16 [768, 768, 128], P('row', ('col', 'depth')), may hold values from -6 to 6
Outputs:
- contact_delta: bfloat16 [768, 768, 128], P('row', ('col', 'depth'))
- alignment_adjoint: float32 [128, 768, 256], P('depth', 'col')
- grad_w_out: float32 [1024, 128], replicated
- grad_b_out: float32 [128], replicated
All inputs are finite; a program needn't handle non-finite values.
Results may differ from a plain program's by a relative error of at most 0.007.
Values may be sent and summed in bfloat16 or wider, within the bound.
No kernel may reach another device: no remote copies, remote signals or barrier semaphores. Data moves between devices by JAX's collectives and lax.ppermute only.
A program may use at most 128 MiB of HBM per device.

v0:
```python
import jax
import jax.numpy as jnp
from jax import lax
from jax.sharding import PartitionSpec as P

epsilon = 1e-05


def in_one(arrays, axis):
    vector, at, gathered = (jnp.concatenate([a.reshape(-1) for a in arrays]), 0, [])
    running = lax.psum(vector, axis)
    for a in arrays:
        gathered.append(running[at : at + a.size].reshape(a.shape))
        at += a.size
    return tuple(gathered)


def broadcast(shard, axis, root):
    return lax.dynamic_index_in_dim(lax.all_gather(shard, axis), root, 0, keepdims=False)


def copy_for_each(shard, axis):
    copies = jnp.broadcast_to(shard, (lax.axis_size(axis), *shard.shape))
    return lax.all_to_all(copies, axis, split_axis=0, concat_axis=0, tiled=True)


def of_everyone(shard, axis):
    everything = copy_for_each(shard, axis)
    return jnp.sum(everything, axis=0)


def standardize_channels(values):
    centre = jnp.mean(values, axis=-1, keepdims=True)
    spread = jnp.mean(jnp.square(values - centre), axis=-1, keepdims=True)
    return (values - centre) * lax.rsqrt(spread + epsilon)


def body(alignment_matrix, twin_linear_matrix, final_matrix, final_offset, adjoint_incoming):
    alignment_share, amino_share, discarded_item = alignment_matrix.shape
    latent_features = twin_linear_matrix.shape[1] // 2
    row_count = lax.axis_size("row")
    col_count = lax.axis_size("col")
    depth_count = lax.axis_size("depth")
    crop_length = amino_share * col_count
    block_i = crop_length // row_count
    quarter = amino_share // depth_count
    row_idx = lax.axis_index("row")
    col_idx = lax.axis_index("col")
    standardized_alignment, standardize_backprop = jax.vjp(
        standardize_channels, alignment_matrix.astype(jnp.float32)
    )
    normed = standardized_alignment.astype(jnp.bfloat16)
    panels = jnp.dot(normed, twin_linear_matrix, preferred_element_type=jnp.float32).astype(
        jnp.bfloat16
    )
    left_local = panels[..., :latent_features]
    right_local = panels[..., latent_features:]
    left_every = lax.all_gather(left_local, "col", axis=1, tiled=True)
    left_rows = lax.dynamic_slice_in_dim(left_every, row_idx * block_i, block_i, 1)
    left_seqs = lax.all_gather(left_rows, "depth", axis=0, tiled=True)
    right_seqs = lax.all_to_all(right_local, "depth", split_axis=1, concat_axis=0, tiled=True)
    seq_count = left_seqs.shape[0]
    summed = jnp.einsum(
        "sje,sic->jice", right_seqs, left_seqs, preferred_element_type=jnp.float32
    ).reshape(quarter, block_i, latent_features * latent_features)
    outer_mean = (summed / seq_count).astype(jnp.bfloat16)
    pair_cols = jnp.dot(outer_mean, final_matrix, preferred_element_type=jnp.float32) + final_offset
    contact_delta = jnp.transpose(pair_cols, (1, 0, 2)).astype(jnp.bfloat16)
    adjoint_kronecker = (
        jnp.einsum(
            "gtz,vz->gtv", adjoint_incoming, final_matrix, preferred_element_type=jnp.float32
        )
        / seq_count
    ).astype(jnp.bfloat16)
    grad_four = adjoint_kronecker.reshape(block_i, quarter, latent_features, latent_features)
    adjoint_leftside = jnp.einsum(
        "ijce,sje->sic", grad_four, right_seqs, preferred_element_type=jnp.float32
    )
    grad_right = jnp.einsum(
        "ijce,sic->sje", grad_four, left_seqs, preferred_element_type=jnp.float32
    )
    w_local = jnp.einsum(
        "jif,ijo->fo", outer_mean, adjoint_incoming, preferred_element_type=jnp.float32
    )
    b_local = jnp.sum(adjoint_incoming.astype(jnp.float32), axis=(0, 1))
    weight_gradient, bias_gradient = in_one((w_local, b_local), ("row", "col", "depth"))
    left_back, right_back = (
        lax.all_to_all(adjoint_leftside, "depth", split_axis=0, concat_axis=1, tiled=True),
        lax.all_to_all(grad_right, "depth", split_axis=0, concat_axis=1, tiled=True),
    )
    left_back = jnp.sum(
        left_back.reshape(alignment_share, depth_count, block_i, latent_features), axis=1
    )
    left_summed = lax.psum(left_back, "col")
    owner_row = col_idx * amino_share // block_i
    left_full = broadcast(left_summed.astype(jnp.bfloat16), "row", owner_row).astype(
        left_summed.dtype
    )
    right_full = of_everyone(right_back, "row")
    both_grads = jnp.concatenate([left_full, right_full], axis=-1)
    grad_panels = both_grads.astype(jnp.bfloat16)
    standardized_adjoint = jnp.einsum(
        "slk,mk->slm", grad_panels, twin_linear_matrix, preferred_element_type=jnp.float32
    )
    alignment_adjoint = standardize_backprop(standardized_adjoint)[0]
    return (
        contact_delta,
        alignment_adjoint,
        weight_gradient / crop_length,
        bias_gradient / crop_length,
    )


def solution(mesh):
    in_specs = (P("depth", "col", None), P(), P(), P(), P("row", ("col", "depth"), None))
    out_specs = (P("row", ("col", "depth"), None), P("depth", "col", None), P(), P())
    return jax.shard_map(body, mesh=mesh, in_specs=in_specs, out_specs=out_specs, check_vma=False)
```

profile of v0, /device:TPU:1, one launch (start us, length us, event | category | flops | bytes accessed | tf_op | source)
XLA Modules:
  0.0 472.1 jit_solution(5661845479301086679)
XLA Ops:
  18.8 5.0 %all-to-all-start = ((bf16[4,2,12288]{2,1,0:T(2,128)(2,1)}), bf16[4,2,12288]{2,1,0:T(2,128)(2,1)S(1)}, u32[]{:S(2)}, u32[]{:S(2)}) async-start(bf16[4,2,12288]{2,1,0:T(2,128)(2,1)} %reshape.73), calls=%async_computation | async-start | bytes 393216 | tf_op jit(solution)/shard_map/all_to_all | solution.py:61
  23.8 3.5 multiply_convert_fusion.1
  27.3 8.5 %copy.39 = bf16[96,24,1024]{0,2,1:T(8,128)(2,1)} copy(bf16[96,24,1024]{2,1,0:T(8,128)(2,1)} %multiply_convert_fusion.1) | data formatting | bytes 9437184 | tf_op jit(solution)/shard_map/convert_element_type | solution.py:74
  37.9 5.1 %convolution_bitcast_fusion.1 = f32[128,96,32]{0,1,2:T(8,128)S(1)} fusion(bf16[96,24,32,32]{0,3,2,1:T(8,128)(2,1)} %bitcast.63, bf16[128,24,32,1]{0,2,1,3:T(8,128)(2,1)} %reshape.66), kind=kOutput, calls=%fused_computation.20 | convolution fusion | flops 603979776 | bytes 6488064 | tf_op jit(solution)/shard_map/ijce,sje->sic/dot_general | solution.py:76
  44.9 4.8 %all-to-all-start.1 = ((f32[128,96,32]{1,2,0:T(8,128)}), f32[128,96,32]{1,2,0:T(8,128)}, u32[]{:S(2)}, u32[]{:S(2)}) async-start(f32[128,96,32]{1,2,0:T(8,128)} %copy.41), calls=%async_computation.1 | async-start | bytes 4194304 | tf_op jit(solution)/shard_map/all_to_all | solution.py:88
  50.0 24.5 %all-to-all-done.1 = f32[128,96,32]{1,2,0:T(8,128)} async-done(((f32[128,96,32]{1,2,0:T(8,128)}), f32[128,96,32]{1,2,0:T(8,128)}, u32[]{:S(2)}, u32[]{:S(2)}) %all-to-all-start.1) | async-done | bytes 1572896 | tf_op jit(solution)/shard_map/all_to_all | solution.py:88
  74.6 2.7 reduce_sum.82
  77.3 13.4 %all-gather.4.cloned.1.call-done = bf16[32,768,32]{2,0,1:T(8,128)(2,1)} async-done(((bf16[32,96,32]{2,0,1:T(8,128)(2,1)}), bf16[32,768,32]{2,0,1:T(8,128)(2,1)}) %all-gather.4.cloned.1.call-update) | async-done | bytes 1572880 | tf_op jit(solution)/shard_map/all_gather | solution.py:58
  92.6 13.8 %all_gather.13 = bf16[128,96,32]{1,2,0:T(8,128)(2,1)S(1)} all-gather(bf16[32,96,32]{1,2,0:T(8,128)(2,1)S(1)} %copy.32), channel_id=1, replica_groups=mesh['row'=8,'col'=8,'depth'=4] {'depth'}, dimensions={0}, use_global_device_ids=true | all-gather | bytes 983040 | tf_op jit(solution)/shard_map/all_gather | solution.py:60
  106.4 5.0 %convolution_bitcast_fusion.2 = f32[128,24,32]{0,2,1:T(8,128)S(1)} fusion(bf16[96,24,32,32]{0,3,2,1:T(8,128)(2,1)} %bitcast.64, bf16[128,96,32]{1,2,0:T(8,128)(2,1)S(1)} %all_gather.13), kind=kOutput, calls=%fused_computation.25 | convolution fusion | flops 603979776 | bytes 5898240 | tf_op jit(solution)/shard_map/ijce,sic->sje/dot_general | solution.py:79
  115.5 2.8 reshape.75
  118.3 3.5 all-to-all-start.2
  121.8 9.1 %fusion = bf16[24,96,32,32]{3,2,0,1:T(8,128)(2,1)} fusion(bf16[128,96,32,1]{0,2,3,1:T(8,128)(2,1)S(1)} %copy.48, bf16[128,24,32,1]{0,2,1,3:T(8,128)(2,1)S(1)} %copy-done.7), kind=kOutput, calls=%fused_computation.1 | convolution fusion | flops 608698368 | bytes 5701632 | tf_op jit(solution)/shard_map/sje,sic->jice/dot_general | solution.py:63
  130.9 20.1 %copy.37 = bf16[24,96,32,32]{1,3,2,0:T(8,128)(2,1)} copy(bf16[24,96,32,32]{3,2,0,1:T(8,128)(2,1)} %fusion) | data formatting | bytes 9437184 | tf_op jit(solution)/shard_map/convert_element_type | solution.py:66
  151.5 2.5 reduce.2
  159.8 2.5 broadcast_in_dim.4
  162.3 4.7 all-to-all-start.3
  167.3 4.3 convolution_bitcast_fusion
  172.6 66.0 %all-reduce.4 = bf16[32,96,32]{1,2,0:T(8,128)(2,1)} all-reduce(f32[32,96,32]{1,2,0:T(8,128)S(1)} %copy-done.6), channel_id=1, replica_groups=mesh['row'=8,'col'=8,'depth'=4] {'col'}, use_global_device_ids=true, to_apply=%region_3.0 | all-reduce | flops 98304 | bytes 589824 | tf_op jit(solution)/shard_map/psum | solution.py:94
  238.7 4.6 fusion.19
  244.3 205.4 %all-reduce.3.cloned.1.call-done = f32[131200]{0:T(1024)} async-done(((f32[131200]{0:T(1024)}), f32[131200]{0:T(1024)}) %all-reduce.3.cloned.1.call-update) | async-done | bytes 524816 | tf_op jit(solution)/shard_map/psum | solution.py:11
  453.8 2.8 reduce_sum.83
  456.6 3.2 multiply_reduce_fusion
  461.5 3.2 fusion.7
  (60 shorter events, 35.2 us)
Async XLA Ops:
  8.0 15.8 %copy-start = (bf16[1024,128]{1,0:T(8,128)(2,1)S(1)}, bf16[1024,128]{1,0:T(8,128)(2,1)}, u32[]{:S(2)}) copy-start(bf16[1024,128]{1,0:T(8,128)(2,1)} %param.7) | copy-start | bytes 786436
  8.0 4.7 copy-start.1
  8.0 4.7 copy-start.8
  8.0 82.6 %all-gather.4.cloned.1.call-start = ((), (), s32[]{:S(2)}) async-start(), calls=%async_computation.4 | async-start | bytes 7077888 | tf_op jit(solution)/shard_map/all_gather | solution.py:58
  14.1 9.8 %copy-start.3 = (bf16[96,24,128]{2,1,0:T(8,128)(2,1)S(1)}, bf16[96,24,128]{2,1,0:T(8,128)(2,1)}, u32[]{:S(2)}) copy-start(bf16[96,24,128]{2,1,0:T(8,128)(2,1)} %param.9) | copy-start | bytes 1769476
  18.8 17.0 %all-to-all-start = ((bf16[4,2,12288]{2,1,0:T(2,128)(2,1)}), bf16[4,2,12288]{2,1,0:T(2,128)(2,1)S(1)}, u32[]{:S(2)}, u32[]{:S(2)}) async-start(bf16[4,2,12288]{2,1,0:T(2,128)(2,1)} %reshape.73), calls=%async_computation | async-start | bytes 393216 | tf_op jit(solution)/shard_map/all_to_all | solution.py:61
  44.9 4.8 %copy-start.4 = (bf16[96,24,128]{2,1,0:T(8,128)(2,1)S(1)}, bf16[96,24,128]{2,1,0:T(8,128)(2,1)}, u32[]{:S(2)}) copy-start(bf16[96,24,128]{2,1,0:T(8,128)(2,1)} %param.9) | copy-start | bytes 1769476
  44.9 29.7 %all-to-all-start.1 = ((f32[128,96,32]{1,2,0:T(8,128)}), f32[128,96,32]{1,2,0:T(8,128)}, u32[]{:S(2)}, u32[]{:S(2)}) async-start(f32[128,96,32]{1,2,0:T(8,128)} %copy.41), calls=%async_computation.1 | async-start | bytes 4194304 | tf_op jit(solution)/shard_map/all_to_all | solution.py:88
  106.4 5.0 %copy-start.2 = (bf16[128,96,32]{1,2,0:T(8,128)(2,1)}, bf16[128,96,32]{1,2,0:T(8,128)(2,1)S(1)}, u32[]{:S(2)}) copy-start(bf16[128,96,32]{1,2,0:T(8,128)(2,1)S(1)} %all_gather.13) | copy-start | bytes 2359300
  111.4 10.4 %copy-start.7 = (bf16[128,24,32,1]{0,2,1,3:T(8,128)(2,1)S(1)}, bf16[128,24,32,1]{0,2,1,3:T(8,128)(2,1)}, u32[]{:S(2)}) copy-start(bf16[128,24,32,1]{0,2,1,3:T(8,128)(2,1)} %reshape.66) | copy-start | bytes 589828
  118.3 32.7 %all-to-all-start.2 = ((f32[4,1,24576]{2,1,0:T(1,128)}), f32[4,1,24576]{2,1,0:T(1,128)S(1)}, u32[]{:S(2)}, u32[]{:S(2)}) async-start(f32[4,1,24576]{2,1,0:T(1,128)} %reshape.75), calls=%async_computation.2 | async-start | bytes 786432 | tf_op jit(solution)/shard_map/all_to_all | solution.py:89
  162.3 5.0 %copy-start.5 = (bf16[96,24,128]{2,1,0:T(8,128)(2,1)S(1)}, bf16[96,24,128]{2,1,0:T(8,128)(2,1)}, u32[]{:S(2)}) copy-start(bf16[96,24,128]{2,1,0:T(8,128)(2,1)} %param.9) | copy-start | bytes 1769476
  162.3 291.5 %all-to-all-start.3 = ((f32[8,32,96,32]{2,3,1,0:T(8,128)}), f32[8,32,96,32]{2,3,1,0:T(8,128)}, u32[]{:S(2)}, u32[]{:S(2)}) async-start(f32[8,32,96,32]{2,3,1,0:T(8,128)} %broadcast_in_dim.4), calls=%async_computation.3 | async-start | bytes 8388608 | tf_op jit(solution)/shard_map/all_to_all | solution.py:24
  167.0 282.8 %all-reduce.3.cloned.1.call-start = ((), (), s32[]{:S(2)}) async-start(), calls=%async_computation.5 | async-start | bytes 1056768 | tf_op jit(solution)/shard_map/psum | solution.py:11
  167.3 5.3 %copy-start.6 = (f32[32,96,32]{1,2,0:T(8,128)S(1)}, f32[32,96,32]{1,2,0:T(8,128)}, u32[]{:S(2)}) copy-start(f32[32,96,32]{1,2,0:T(8,128)} %reduce_sum.82) | copy-start | bytes 1179652
  167.3 71.4 %copy-start.9 = (f32[128]{0:T(128)S(1)}, f32[128]{0:T(128)}, u32[]{:S(2)}) copy-start(f32[128]{0:T(128)} %param.8) | copy-start | bytes 1540
  172.5 280.3 %all-gather.6.cloned.1.call-start = ((), (), s32[]{:S(2)}) async-start(), calls=%async_computation.6 | async-start | bytes 2359296 | tf_op jit(solution)/shard_map/all_gather | solution.py:19
Sparse Core Ops, SparseCore 0:
  16.3 74.2 all-gather.3
  173.9 275.8 all-reduce.2
Sparse Core Ops, SparseCore 1:
  238.7 60.2 all-gather.5
where the time goes:
time: 474 us; the launch traced here: 472 us
  waiting for transfers between devices  243 us (51%)
  blocking collectives  79.8 us (17%)
  local copies, waits for them, and re-layouts  57 us (12%)
  matrix products  36.2 us (8%)
  other arithmetic  21.6 us (5%)
  starting transfers between devices  18.3 us (4%)
  between operations  15.8 us (3%)
    psum x1, waiting for transfers between devices, in_one(): running = lax.psum(vector, axis)  205 us
    psum x1, blocking collectives, body(): left_summed = lax.psum(left_back, 'col')  66 us
    all_to_all x1, waiting for transfers between devices, body(): lax.all_to_all(adjoint_leftside, 'depth', split_axis=0, concat_axis=1, ti...  24.5 us
    convert_element_type x1, local copies, waits for them, and re-layouts, body(): outer_mean = (summed / seq_count).astype(jnp.bfloat16)  20.1 us
    all_gather x1, blocking collectives, body(): left_seqs = lax.all_gather(left_rows, 'depth', axis=0, tiled=True)  13.8 us
    all_gather x1, waiting for transfers between devices, body(): left_every = lax.all_gather(left_local, 'col', axis=1, tiled=True)  13.4 us
  transfers between devices with their start and end apart: 7, of which 3 were waited for; matrix products, arithmetic and copies ran while one was open for 15% of the time, Pallas kernels for 0%

commit v1 on v0

--- a/solution.py
+++ b/solution.py
@@ -91,7 +91,7 @@
     left_back = jnp.sum(
         left_back.reshape(alignment_share, depth_count, block_i, latent_features), axis=1
     )
-    left_summed = lax.psum(left_back, "col")
+    left_summed = jnp.sum(lax.all_gather(left_back, "col"), axis=0)
     owner_row = col_idx * amino_share // block_i
     left_full = broadcast(left_summed.astype(jnp.bfloat16), "row", owner_row).astype(
         left_summed.dtype

time: 474 us -> 498 us (1.051)
  waiting for transfers between devices: 243 us -> 307 us
  blocking collectives: 79.8 us -> 43 us
    psum x1 -> x0, blocking collectives: 66 us -> none  [body(): left_summed = lax.psum(left_back, 'col')]
    all_gather x1, waiting for transfers between devices: 0.01 us -> 47 us  [broadcast(): lax.all_gather(shard, axis)]
    psum x1, waiting for transfers between devices: 205 us -> 243 us  [in_one(): running = lax.psum(vector, axis)]
    all_to_all x0 -> x1, blocking collectives: none -> 29.1 us  [body(): lax.all_to_all(adjoint_leftside, 'depth', split_axis=0, concat_axis=1, ti...]
    all_to_all x1 -> x0, waiting for transfers between devices: 24.5 us -> none  [body(): lax.all_to_all(adjoint_leftside, 'depth', split_axis=0, concat_axis=1, ti...]
  transfers between devices with their start and end apart: 7 -> 7, of which waited for: 3 -> 4; matrix products, arithmetic and copies ran while one was open for 15% -> 20% of each run, Pallas kernels for 0% -> 0%
where the time goes in v1:
time: 498 us; the launch traced here: 497 us
  waiting for transfers between devices  307 us (62%)
  local copies, waits for them, and re-layouts  57.8 us (12%)
  blocking collectives  43 us (9%)
  matrix products  36.5 us (7%)
  other arithmetic  25.4 us (5%)
  between operations  14 us (3%)
  starting transfers between devices  13.5 us (3%)
    psum x1, waiting for transfers between devices, in_one(): running = lax.psum(vector, axis)  243 us
    all_gather x1, waiting for transfers between devices, broadcast(): lax.all_gather(shard, axis)  47 us
    all_to_all x1, blocking collectives, body(): lax.all_to_all(adjoint_leftside, 'depth', split_axis=0, concat_axis=1, ti...  29.1 us
    convert_element_type x1, local copies, waits for them, and re-layouts, body(): outer_mean = (summed / seq_count).astype(jnp.bfloat16)  20.2 us
    all_gather x1, waiting for transfers between devices, body(): left_every = lax.all_gather(left_local, 'col', axis=1, tiled=True)  13.9 us
    all_gather x1, blocking collectives, body(): left_seqs = lax.all_gather(left_rows, 'depth', axis=0, tiled=True)  13.9 us
  transfers between devices with their start and end apart: 7, of which 4 were waited for; matrix products, arithmetic and copies ran while one was open for 20% of the time, Pallas kernels for 0%

profile of v1, /device:TPU:1, one launch (start us, length us, event | category | flops | bytes accessed | tf_op | source)
XLA Modules:
  0.0 496.8 jit_solution(4450139544239095690)
XLA Ops:
  18.0 5.0 %all-to-all-start = ((bf16[4,2,12288]{2,1,0:T(2,128)(2,1)}), bf16[4,2,12288]{2,1,0:T(2,128)(2,1)S(1)}, u32[]{:S(2)}, u32[]{:S(2)}) async-start(bf16[4,2,12288]{2,1,0:T(2,128)(2,1)} %reshape.82), calls=%async_computation | async-start | bytes 393216 | tf_op jit(solution)/shard_map/all_to_all | solution.py:61
  23.0 3.5 multiply_convert_fusion.1
  26.5 8.5 %copy.39 = bf16[96,24,1024]{0,2,1:T(8,128)(2,1)} copy(bf16[96,24,1024]{2,1,0:T(8,128)(2,1)} %multiply_convert_fusion.1) | data formatting | bytes 9437184 | tf_op jit(solution)/shard_map/convert_element_type | solution.py:74
  37.1 5.1 %convolution_bitcast_fusion.1 = f32[128,96,32]{0,1,2:T(8,128)S(1)} fusion(bf16[96,24,32,32]{0,3,2,1:T(8,128)(2,1)} %bitcast.64, bf16[128,24,32,1]{0,2,1,3:T(8,128)(2,1)} %reshape.75), kind=kOutput, calls=%fused_computation.20 | convolution fusion | flops 603979776 | bytes 6488064 | tf_op jit(solution)/shard_map/ijce,sje->sic/dot_general | solution.py:76
  44.1 29.1 %all_to_all.53 = f32[128,96,32]{1,2,0:T(8,128)} all-to-all(f32[128,96,32]{1,2,0:T(8,128)} %copy.41), channel_id=1, replica_groups=mesh['row'=8,'col'=8,'depth'=4] {'depth'}, dimensions={0} | all-to-all | bytes 3145728 | tf_op jit(solution)/shard_map/all_to_all | solution.py:88
  73.2 2.7 reduce_sum.91
  75.9 13.9 %all-gather.6.cloned.1.call-done = bf16[32,768,32]{2,0,1:T(8,128)(2,1)} async-done(((bf16[32,96,32]{2,0,1:T(8,128)(2,1)}), bf16[32,768,32]{2,0,1:T(8,128)(2,1)}) %all-gather.6.cloned.1.call-update) | async-done | bytes 1572880 | tf_op jit(solution)/shard_map/all_gather | solution.py:58
  91.8 13.9 %all_gather.17 = bf16[128,96,32]{1,2,0:T(8,128)(2,1)S(1)} all-gather(bf16[32,96,32]{1,2,0:T(8,128)(2,1)S(1)} %copy.32), channel_id=1, replica_groups=mesh['row'=8,'col'=8,'depth'=4] {'depth'}, dimensions={0}, use_global_device_ids=true | all-gather | bytes 983040 | tf_op jit(solution)/shard_map/all_gather | solution.py:60
  106.7 5.3 %convolution_bitcast_fusion.2 = f32[128,24,32]{0,2,1:T(8,128)} fusion(bf16[96,24,32,32]{0,3,2,1:T(8,128)(2,1)} %bitcast.65, bf16[128,96,32]{1,2,0:T(8,128)(2,1)S(1)} %all_gather.17), kind=kOutput, calls=%fused_computation.25 | convolution fusion | flops 603979776 | bytes 5898240 | tf_op jit(solution)/shard_map/ijce,sic->sje/dot_general | solution.py:79
  115.0 3.5 all-to-all-start.2
  122.3 2.6 all-to-all-done.2
  128.9 2.9 copy.44
  134.1 2.6 broadcast_in_dim.4
  136.7 4.7 all-to-all-start.3
  141.7 9.1 %fusion = bf16[24,96,32,32]{3,2,0,1:T(8,128)(2,1)} fusion(bf16[128,96,32,1]{0,2,3,1:T(8,128)(2,1)S(1)} %copy.48, bf16[128,24,32,1]{0,2,1,3:T(8,128)(2,1)S(1)} %copy-done.5), kind=kOutput, calls=%fused_computation.1 | convolution fusion | flops 608698368 | bytes 5701632 | tf_op jit(solution)/shard_map/sje,sic->jice/dot_general | solution.py:63
  150.8 20.2 %copy.37 = bf16[24,96,32,32]{1,3,2,0:T(8,128)(2,1)} copy(bf16[24,96,32,32]{3,2,0,1:T(8,128)(2,1)} %fusion) | data formatting | bytes 9437184 | tf_op jit(solution)/shard_map/convert_element_type | solution.py:66
  171.0 4.3 convolution_bitcast_fusion
  176.2 3.5 reduce_sum.92
  179.8 4.6 fusion.19
  185.4 242.9 %all-reduce.2.cloned.1.call-done = f32[131200]{0:T(1024)} async-done(((f32[131200]{0:T(1024)}), f32[131200]{0:T(1024)}) %all-reduce.2.cloned.1.call-update) | async-done | bytes 524816 | tf_op jit(solution)/shard_map/psum | solution.py:11
  431.4 2.8 reduce_sum.93
  434.2 47.0 %all-gather.10.cloned.1.call-done = bf16[256,96,32]{1,2,0:T(8,128)(2,1)} async-done(((bf16[32,96,32]{1,2,0:T(8,128)(2,1)}), bf16[256,96,32]{1,2,0:T(8,128)(2,1)}) %all-gather.10.cloned.1.call-update) | async-done | bytes 1572880 | tf_op jit(solution)/shard_map/all_gather | solution.py:19
  482.2 3.2 multiply_reduce_fusion
  487.1 3.2 fusion.7
  (58 shorter events, 38.7 us)
Async XLA Ops:
  7.2 15.8 %copy-start = (bf16[1024,128]{1,0:T(8,128)(2,1)S(1)}, bf16[1024,128]{1,0:T(8,128)(2,1)}, u32[]{:S(2)}) copy-start(bf16[1024,128]{1,0:T(8,128)(2,1)} %param.7) | copy-start | bytes 786436
  7.2 4.7 copy-start.1
  7.2 4.7 copy-start.6
  7.2 82.6 %all-gather.6.cloned.1.call-start = ((), (), s32[]{:S(2)}) async-start(), calls=%async_computation.4 | async-start | bytes 7077888 | tf_op jit(solution)/shard_map/all_gather | solution.py:58
  13.2 9.8 %copy-start.3 = (bf16[96,24,128]{2,1,0:T(8,128)(2,1)S(1)}, bf16[96,24,128]{2,1,0:T(8,128)(2,1)}, u32[]{:S(2)}) copy-start(bf16[96,24,128]{2,1,0:T(8,128)(2,1)} %param.9) | copy-start | bytes 1769476
  18.0 17.0 %all-to-all-start = ((bf16[4,2,12288]{2,1,0:T(2,128)(2,1)}), bf16[4,2,12288]{2,1,0:T(2,128)(2,1)S(1)}, u32[]{:S(2)}, u32[]{:S(2)}) async-start(bf16[4,2,12288]{2,1,0:T(2,128)(2,1)} %reshape.82), calls=%async_computation | async-start | bytes 393216 | tf_op jit(solution)/shard_map/all_to_all | solution.py:61
  23.0 153.2 %all-gather.8.cloned.1.call-start = ((), (), s32[]{:S(2)}) async-start(), calls=%async_computation.6 | async-start | bytes 4718592 | tf_op jit(solution)/shard_map/all_gather | solution.py:94
  105.8 1.0 copy-start.2
  115.0 9.8 %all-to-all-start.2 = ((f32[4,1,24576]{2,1,0:T(1,128)}), f32[4,1,24576]{2,1,0:T(1,128)S(1)}, u32[]{:S(2)}, u32[]{:S(2)}) async-start(f32[4,1,24576]{2,1,0:T(1,128)} %reshape.84), calls=%async_computation.2 | async-start | bytes 786432 | tf_op jit(solution)/shard_map/all_to_all | solution.py:89
  136.7 5.0 %copy-start.5 = (bf16[128,24,32,1]{0,2,1,3:T(8,128)(2,1)S(1)}, bf16[128,24,32,1]{0,2,1,3:T(8,128)(2,1)}, u32[]{:S(2)}) copy-start(bf16[128,24,32,1]{0,2,1,3:T(8,128)(2,1)} %reshape.75) | copy-start | bytes 589828
  136.7 294.7 %all-to-all-start.3 = ((f32[8,32,96,32]{2,3,1,0:T(8,128)}), f32[8,32,96,32]{2,3,1,0:T(8,128)}, u32[]{:S(2)}, u32[]{:S(2)}) async-start(f32[8,32,96,32]{2,3,1,0:T(8,128)} %broadcast_in_dim.4), calls=%async_computation.3 | async-start | bytes 8388608 | tf_op jit(solution)/shard_map/all_to_all | solution.py:24
  141.5 286.9 %all-reduce.2.cloned.1.call-start = ((), (), s32[]{:S(2)}) async-start(), calls=%async_computation.5 | async-start | bytes 1056768 | tf_op jit(solution)/shard_map/psum | solution.py:11
  150.8 20.2 %copy-start.4 = (bf16[96,24,128]{2,1,0:T(8,128)(2,1)S(1)}, bf16[96,24,128]{2,1,0:T(8,128)(2,1)}, u32[]{:S(2)}) copy-start(bf16[96,24,128]{2,1,0:T(8,128)(2,1)} %param.9) | copy-start | bytes 1769476
  175.3 4.5 copy-start.7
  176.1 305.1 %all-gather.10.cloned.1.call-start = ((), (), s32[]{:S(2)}) async-start(), calls=%async_computation.7 | async-start | bytes 2359296 | tf_op jit(solution)/shard_map/all_gather | solution.py:19
Sparse Core Ops, SparseCore 0:
  15.5 74.3 all-gather.5
  92.3 51.3 all-gather.7
  176.3 252.0 all-reduce.1
  430.0 51.2 all-gather.9
